TPU v7x, 256 devices: a whole 4x4x8 slice. The times are simulated.
256 devices in a mesh: row: 16 (over y_lo, x, core), col: 16 (over z, y_hi).
Axes of the slice: x: 4, y: 4 (y_hi: 2, y_lo: 2; y = y_hi * 2 + y_lo), z: 8, core: 2. Of those that a mesh axis runs over, the one named last changes fastest.
Arguments:
- tokens: bfloat16 [16, 16, 736, 1024], P('row', 'col'), may hold values from -6 to 6
- local_params: bfloat16 [16, 16, 2, 1024, 1024], P('row', 'col'), may hold values from -0.1875 to 0.1875
- outer_params: float32 [2, 16, 16, 16, 4, 1024], P(None, None, 'col', 'row'), may hold values from -0.1875 to 0.1875
- momentum: float32 [2, 16, 16, 16, 4, 1024], P(None, None, 'col', 'row'), may hold values from -0.1875 to 0.1875
- table: int32 [16, 16], replicated, may hold values from 0 to 15, each once within a row
- counts: int32 [16, 16], replicated, may hold values from 64 to 4095
Outputs:
- path_params: bfloat16 [16, 16, 2, 1024, 1024], P('row', 'col')
- outer_out: float32 [2, 16, 16, 16, 4, 1024], P(None, None, 'col', 'row')
- momentum_out: float32 [2, 16, 16, 16, 4, 1024], P(None, None, 'col', 'row')
- hidden_out: bfloat16 [16, 16, 736, 1024], P('row', 'col')
Inputs may be any that keep to these rules, and one draw needn't show every extreme that they name: Each row of the table names every level-two module exactly once.
All inputs are finite; a program needn't handle non-finite values.
Results may differ from a plain program's by a relative error of at most 0.01.
Values may be sent and summed in bfloat16 or wider, within the bound.
No kernel may reach another device: no remote copies, remote signals or barrier semaphores. Data moves between devices by JAX's collectives and lax.ppermute only.
A program may use at most 64 MiB of HBM per device.

v0:
```python
import jax
import jax.numpy as jnp
from jax import lax
from jax.sharding import PartitionSpec as P


def cut_along(shard, dim, count):
    before, after = (shard.shape[:dim], shard.shape[dim + 1 :])
    return jnp.moveaxis(shard.reshape(*before, count, -1, *after), dim, 0)


def sum_at_owner(shard, axis, dim):
    blocks = cut_along(shard, dim, lax.axis_size(axis))
    arrived = lax.all_to_all(blocks, axis, split_axis=0, concat_axis=0, tiled=True)
    return arrived.astype(jnp.float32).sum(axis=0)


def outer_round(scaled, outer, moment, my_row, inverse):
    layers = scaled.shape[0]
    width = scaled.shape[-1]
    n_col = lax.axis_size("col")
    pieces = scaled.reshape(layers, n_col, width // n_col, width)
    arrived = lax.all_to_all(pieces, "col", split_axis=1, concat_axis=1, tiled=True)
    ordered = jnp.take(arrived, inverse, axis=1)
    summed = sum_at_owner(ordered, "row", 2)
    delta = outer - summed
    moment_new = 0.9 * moment + delta
    outer_new = outer - 0.7 * (delta + 0.9 * moment_new)
    whole = lax.all_gather(outer_new.astype(jnp.bfloat16), "row", axis=2, tiled=True)
    chosen = jnp.take(whole, my_row, axis=1)
    returned = lax.all_to_all(chosen, "col", split_axis=1, concat_axis=1, tiled=True)
    return (outer_new, moment_new, returned.reshape(layers, width, width))


def micro_step(tokens_path, params_path):
    state = tokens_path.astype(jnp.float32)
    for layer in range(params_path.shape[0]):
        scale = lax.rsqrt(jnp.mean(state * state, axis=-1, keepdims=True) + 1e-06)
        normed = (state * scale).astype(jnp.bfloat16)
        mixed = jnp.dot(normed, params_path[layer], preferred_element_type=jnp.float32)
        state = state + jax.nn.gelu(mixed, approximate=False)
    return state.astype(jnp.bfloat16)


def on_device(tokens, local_params, outer_params, momentum, table, counts):
    row_index = lax.axis_index("row")
    col_index = lax.axis_index("col")
    n_col = table.shape[1]
    ids = jnp.arange(n_col, dtype=jnp.int32)
    matches = (table[:, :, None] == ids[None, None, :]).astype(jnp.float32)
    totals = jnp.sum(counts.astype(jnp.float32)[:, :, None] * matches, axis=(0, 1))
    my_row = lax.dynamic_index_in_dim(table, row_index, 0, keepdims=False)
    count_row = lax.dynamic_index_in_dim(counts, row_index, 0, keepdims=False)
    my_module = lax.dynamic_index_in_dim(my_row, col_index, 0, keepdims=False)
    my_count = lax.dynamic_index_in_dim(count_row, col_index, 0, keepdims=False)
    share = my_count.astype(jnp.float32) / jnp.sum(totals * (ids == my_module).astype(jnp.float32))
    inverse = jnp.sum(ids[:, None] * (my_row[:, None] == ids[None, :]).astype(jnp.int32), axis=0)
    params = local_params[0, 0]
    layers = params.shape[0]
    width = params.shape[-1]
    scaled = (share * params.astype(jnp.float32)).astype(jnp.bfloat16)
    outer = outer_params.reshape(layers, n_col, -1, width)
    moment = momentum.reshape(layers, n_col, -1, width)
    outer_new, moment_new, returned = outer_round(scaled, outer, moment, my_row, inverse)
    hidden = micro_step(tokens[0, 0], params)
    return (
        returned[None, None],
        outer_new.reshape(outer_params.shape),
        moment_new.reshape(momentum.shape),
        hidden[None, None],
    )


def solution(mesh):
    return jax.shard_map(
        on_device,
        mesh=mesh,
        in_specs=(
            P("row", "col", None, None),
            P("row", "col", None, None, None),
            P(None, None, "col", "row", None, None),
            P(None, None, "col", "row", None, None),
            P(),
            P(),
        ),
        out_specs=(
            P("row", "col", None, None, None),
            P(None, None, "col", "row", None, None),
            P(None, None, "col", "row", None, None),
            P("row", "col", None, None),
        ),
        check_vma=False,
    )
```

profile of v0, /device:TPU:1, one launch (start us, length us, event | category | flops | bytes accessed | tf_op | source)
XLA Modules:
  0.0 381.6 jit_solution(6195041350932074072)
XLA Ops:
  7.2 0.7 convert_element_type.53
  7.9 1.3 dynamic_slice.12
  9.1 1.3 dynamic_slice.13
  10.4 0.8 select_reduce_fusion
  11.9 1.2 fusion.49
  13.9 3.3 multiply_convert_fusion
  17.1 2.5 copy.58
  19.6 11.8 %all-to-all-start = ((bf16[2,16,64,1024]{3,2,0,1:T(8,128)(2,1)}), bf16[2,16,64,1024]{3,2,0,1:T(8,128)(2,1)}, u32[]{:S(2)}, u32[]{:S(2)}) async-start(bf16[2,16,64,1024]{3,2,0,1:T(8,128)(2,1)} %copy.58), calls=%async_computation | async-start | bytes 8388608 | tf_op jit(solution)/shard_map/all_to_all | solution.py:23
  31.4 0.0 all-gather.2.cloned.1.call-start
  31.4 0.7 compare_and_fusion
  32.1 0.1 select_reduce_fusion.1
  32.3 97.6 %all-to-all-done = bf16[2,16,64,1024]{3,2,0,1:T(8,128)(2,1)} async-done(((bf16[2,16,64,1024]{3,2,0,1:T(8,128)(2,1)}), bf16[2,16,64,1024]{3,2,0,1:T(8,128)(2,1)}, u32[]{:S(2)}, u32[]{:S(2)}) %all-to-all-start) | async-done | bytes 4194336 | tf_op jit(solution)/shard_map/all_to_all | solution.py:23
  129.9 5.0 %gather_fusion = bf16[16,2,64,1024]{3,2,1,0:T(8,128)(2,1)} fusion(bf16[2,16,64,1024]{3,2,0,1:T(8,128)(2,1)} %all-to-all-done, s32[1024]{0:T(1024)S(1)} %pad_clamp_fusion.1), kind=kCustom, calls=%fused_computation.clone | custom fusion | bytes 8388672 | tf_op jit(solution)/shard_map/jit(_take)/gather | solution.py:24
  134.9 4.7 %select_bitcast_fusion.1 = bf16[2,16,64,1024]{3,2,0,1:T(8,128)(2,1)} fusion(bf16[16,2,64,1024]{3,2,1,0:T(8,128)(2,1)} %gather_fusion, pred[16]{0:T(512)(128)(4,1)S(1)} %compare_and_fusion.1), kind=kLoop, calls=%fused_computation.8 | loop fusion | flops 2097152 | bytes 8388624 | tf_op jit(solution)/shard_map/jit(_take)/select_n | solution.py:24
  139.6 7.2 %reshape.72 = bf16[2,16,16,4,1024]{4,3,2,0,1:T(4,128)(2,1)} reshape(bf16[2,16,64,1024]{3,2,0,1:T(8,128)(2,1)} %select_bitcast_fusion.1) | data formatting | bytes 8388608 | tf_op jit(solution)/shard_map/reshape | solution.py:9
  146.8 4.6 %copy.93 = bf16[2,16,16,4,1024]{4,3,0,1,2:T(4,128)(2,1)S(1)} copy(bf16[2,16,16,4,1024]{4,3,2,0,1:T(4,128)(2,1)} %reshape.72) | data formatting | bytes 8388608 | tf_op jit(solution)/shard_map/reshape | solution.py:9
  151.3 54.5 %all_to_all.15 = bf16[16,2,16,4,1024]{4,3,1,2,0:T(4,128)(2,1)S(1)} all-to-all(bf16[16,2,16,4,1024]{4,3,1,2,0:T(4,128)(2,1)S(1)} %bitcast.75), channel_id=1, replica_groups=mesh['row'=16,'col'=16] {'row'}, dimensions={0} | all-to-all | bytes 8388608 | tf_op jit(solution)/shard_map/all_to_all | solution.py:14
  205.8 0.0 copy-start.1
  205.8 0.0 copy-start.2
  205.8 2.2 convert_reduce_fusion
  208.1 0.0 copy-done.1
  208.1 0.0 copy-done.2
  208.1 0.6 fusion.47
  208.7 0.9 copy.63
  209.6 0.0 all-gather.2.cloned.1.call-update
  209.7 35.8 %all-gather.2.cloned.1.call-done = bf16[2,16,64,1024]{3,1,0,2:T(8,128)(2,1)} async-done(((bf16[2,16,4,1024]{3,1,0,2:T(8,128)(2,1)}), bf16[2,16,64,1024]{3,1,0,2:T(8,128)(2,1)}) %all-gather.2.cloned.1.call-update) | async-done | bytes 4194320 | tf_op jit(solution)/shard_map/all_gather | solution.py:29
  245.5 6.5 %copy.64 = bf16[2,16,64,1024]{3,2,1,0:T(8,128)(2,1)} copy(bf16[2,16,64,1024]{3,1,0,2:T(8,128)(2,1)} %all-gather.2.cloned.1.call-done) | data formatting | bytes 8388608 | tf_op jit(solution)/shard_map/all_gather | solution.py:29
  252.0 4.9 %gather_fusion.1 = bf16[16,2,64,1024]{3,2,1,0:T(8,128)(2,1)} fusion(bf16[2,16,64,1024]{3,2,1,0:T(8,128)(2,1)} %copy.64, s32[1024]{0:T(1024)S(1)} %pad_clamp_fusion), kind=kCustom, calls=%fused_computation.1.clone | custom fusion | bytes 8388672 | tf_op jit(solution)/shard_map/jit(_take)/gather | solution.py:30
  256.9 4.7 %select_bitcast_fusion = bf16[2,16,64,1024]{3,2,0,1:T(8,128)(2,1)} fusion(bf16[16,2,64,1024]{3,2,1,0:T(8,128)(2,1)} %gather_fusion.1, pred[16]{0:T(512)(128)(4,1)S(1)} %get-tuple-element.25), kind=kLoop, calls=%fused_computation.7 | loop fusion | flops 2097152 | bytes 8388624 | tf_op jit(solution)/shard_map/jit(_take)/select_n | solution.py:30
  261.6 0.0 copy-start.3
  261.6 9.2 %all-to-all-start.2 = ((bf16[2,16,64,1024]{3,2,0,1:T(8,128)(2,1)}), bf16[2,16,64,1024]{3,2,0,1:T(8,128)(2,1)}, u32[]{:S(2)}, u32[]{:S(2)}) async-start(bf16[2,16,64,1024]{3,2,0,1:T(8,128)(2,1)} %select_bitcast_fusion), calls=%async_computation.2 | async-start | bytes 8388608 | tf_op jit(solution)/shard_map/all_to_all | solution.py:31
  270.8 0.0 copy-done.3
  270.8 0.4 fusion.2
  271.2 0.0 copy-start
  271.2 10.1 %multiply_reduce_fusion = (f32[736]{0:T(1024)S(1)}, f32[736,1024]{1,0:T(8,128)S(1)}) fusion(bf16[1,1,2,1024,1024]{4,3,2,1,0:T(8,128)(2,1)} %param.9, bf16[1,1,736,1024]{3,2,1,0:T(8,128)(2,1)S(1)} %copy-done.3, f32[736]{0:T(1024)S(1)} %add_rsqrt_fusion.1), kind=kOutput, calls=%fused_computation.35 | convolution fusion | flops 1597013248 | bytes 8133504 | tf_op jit(solution)/shard_map/dot_general | solution.py:40
  281.3 0.0 copy-done
  281.3 9.4 %fusion.36 = bf16[1,1,736,1024]{3,2,1,0:T(8,128)(2,1)} fusion(f32[736,1024]{1,0:T(8,128)S(1)} %get-tuple-element.30, bf16[1,1,2,1024,1024]{4,3,2,1,0:T(8,128)(2,1)S(1)} %copy-done, f32[736]{0:T(1024)S(1)} %add_rsqrt_fusion), kind=kOutput, calls=%fused_computation.62 | convolution fusion | flops 1594753024 | bytes 9637888 | tf_op jit(solution)/shard_map/dot_general | solution.py:40
  290.7 0.7 fusion.48
  291.4 0.8 copy.68
  292.2 0.8 copy.69
  293.0 76.8 %all-to-all-done.2 = bf16[2,16,64,1024]{3,2,0,1:T(8,128)(2,1)} async-done(((bf16[2,16,64,1024]{3,2,0,1:T(8,128)(2,1)}), bf16[2,16,64,1024]{3,2,0,1:T(8,128)(2,1)}, u32[]{:S(2)}, u32[]{:S(2)}) %all-to-all-start.2) | async-done | bytes 4194336 | tf_op jit(solution)/shard_map/all_to_all | solution.py:31
  369.8 4.9 %copy.65 = bf16[2,16,64,1024]{3,2,1,0:T(8,128)(2,1)} copy(bf16[2,16,64,1024]{3,2,0,1:T(8,128)(2,1)} %all-to-all-done.2) | data formatting | bytes 8388608 | tf_op jit(solution)/shard_map/all_to_all | solution.py:31
  (7 shorter events, 0.0 us)
Async XLA Ops:
  19.6 110.3 %all-to-all-start = ((bf16[2,16,64,1024]{3,2,0,1:T(8,128)(2,1)}), bf16[2,16,64,1024]{3,2,0,1:T(8,128)(2,1)}, u32[]{:S(2)}, u32[]{:S(2)}) async-start(bf16[2,16,64,1024]{3,2,0,1:T(8,128)(2,1)} %copy.58), calls=%async_computation | async-start | bytes 8388608 | tf_op jit(solution)/shard_map/all_to_all | solution.py:23
  31.4 214.1 %all-gather.2.cloned.1.call-start = ((), (), s32[]{:S(2)}) async-start(), calls=%async_computation.3 | async-start | bytes 4456448 | tf_op jit(solution)/shard_map/all_gather | solution.py:29
  205.8 2.3 copy-start.1
  205.8 2.3 copy-start.2
  261.6 9.3 %copy-start.3 = (bf16[1,1,736,1024]{3,2,1,0:T(8,128)(2,1)S(1)}, bf16[1,1,736,1024]{3,2,1,0:T(8,128)(2,1)}, u32[]{:S(2)}) copy-start(bf16[1,1,736,1024]{3,2,1,0:T(8,128)(2,1)} %param.8) | copy-start | bytes 4521988
  261.6 108.2 %all-to-all-start.2 = ((bf16[2,16,64,1024]{3,2,0,1:T(8,128)(2,1)}), bf16[2,16,64,1024]{3,2,0,1:T(8,128)(2,1)}, u32[]{:S(2)}, u32[]{:S(2)}) async-start(bf16[2,16,64,1024]{3,2,0,1:T(8,128)(2,1)} %select_bitcast_fusion), calls=%async_computation.2 | async-start | bytes 8388608 | tf_op jit(solution)/shard_map/all_to_all | solution.py:31
  271.2 10.1 %copy-start = (bf16[1,1,2,1024,1024]{4,3,2,1,0:T(8,128)(2,1)S(1)}, bf16[1,1,2,1024,1024]{4,3,2,1,0:T(8,128)(2,1)}, u32[]{:S(2)}) copy-start(bf16[1,1,2,1024,1024]{4,3,2,1,0:T(8,128)(2,1)} %param.9) | copy-start | bytes 12582916
Sparse Core Ops, SparseCore 0:
  209.7 35.6 all-gather.1
where the time goes:
time: 382 us
  waiting for transfers between devices  210 us (55%)
  blocking collectives  54.5 us (14%)
  local copies, waits for them, and re-layouts  40.7 us (11%)
  starting transfers between devices  21.1 us (6%)
  other arithmetic  20.2 us (5%)
  matrix products  19.5 us (5%)
  between operations  15.5 us (4%)
    all_to_all x1, waiting for transfers between devices, outer_round(): lax.all_to_all(pieces, 'col', split_axis=1, concat_axis=1, tiled=True)  97.6 us
    all_to_all x1, waiting for transfers between devices, outer_round(): lax.all_to_all(chosen, 'col', split_axis=1, concat_axis=1, tiled=True)  76.8 us
    all_to_all x1, blocking collectives, sum_at_owner(): lax.all_to_all(blocks, axis, split_axis=0, concat_axis=0, tiled=True)  54.5 us
    all_gather x1, waiting for transfers between devices, outer_round(): lax.all_gather(outer_new.astype(jnp.bfloat16), 'row', axis=2, tiled=True)  35.8 us
    dot_general x2, matrix products, micro_step(): jnp.dot(normed, params_path[layer], preferred_element_type=jnp.float32)  19.5 us
    all_to_all x1, starting transfers between devices, outer_round(): lax.all_to_all(pieces, 'col', split_axis=1, concat_axis=1, tiled=True)  11.8 us
    reshape x2, local copies, waits for them, and re-layouts, cut_along(): return jnp.moveaxis(shard.reshape(*before, count, -1, *after), dim, 0)  11.8 us
    all_to_all x1, starting transfers between devices, outer_round(): lax.all_to_all(chosen, 'col', split_axis=1, concat_axis=1, tiled=True)  9.24 us
  transfers between devices with their start and end apart: 3, of which 3 were waited for; matrix products, arithmetic and copies ran while one was open for 6% of the time, Pallas kernels for 0%

commit v1 on v0

v1 whole, which is shorter than its diff:
```python
import functools

import jax
import jax.numpy as jnp
from jax import lax
from jax.experimental import pallas as pl
from jax.experimental.pallas import tpu as pltpu
from jax.sharding import Mesh
from jax.sharding import PartitionSpec as P

N_CHUNK = 1
PLANE = ("yl", "x", "core", "yh")
F32 = jnp.float32
BF16 = jnp.bfloat16


def cost(flops, bytes_accessed):
    return pl.CostEstimate(flops=flops, bytes_accessed=bytes_accessed, transcendentals=0)


def low_half(shape):
    return lax.broadcasted_iota(jnp.int32, shape, len(shape) - 2) < 4


def swap_halves(first, second):
    mask = low_half(first.shape)
    axis = len(first.shape) - 2
    return (
        jnp.where(mask, first, pltpu.roll(second, 4, axis)),
        jnp.where(mask, pltpu.roll(first, 4, axis), second),
    )


def pack_kernel(place, table, counts, params, *outs):
    ids = table[...]
    tokens = counts[...].astype(F32)
    here = (lax.broadcasted_iota(jnp.int32, ids.shape, 0) == place[0]) & (
        lax.broadcasted_iota(jnp.int32, ids.shape, 1) == place[1]
    )
    module = jnp.sum(jnp.where(here, ids, 0).astype(F32))
    total = jnp.sum(jnp.where(ids.astype(F32) == module, tokens, 0.0), keepdims=True)
    mine = jnp.sum(jnp.where(here, tokens, 0.0), keepdims=True)
    share = mine / total
    width = params.shape[-1] // len(outs)
    for yh in range(2):
        for pair in range(8):
            rows = pl.ds(yh * 64 + pair * 8, 8)
            for h, out in enumerate(outs):
                cols = pl.ds(h * width, width)
                first = params[0, 0, rows, cols].astype(F32) * share
                second = params[1, 0, rows, cols].astype(F32) * share
                even, odd = swap_halves(first, second)
                out[(2 * pair) * 2 + yh, 0] = even.astype(BF16)
                out[(2 * pair + 1) * 2 + yh, 0] = odd.astype(BF16)


def pack(place, table, counts, params):
    layers, width = params.shape[0], params.shape[-1]
    view = params.reshape(layers, 8, 128, width)
    part = width // N_CHUNK
    return pl.pallas_call(
        pack_kernel,
        name="pack",
        grid_spec=pltpu.PrefetchScalarGridSpec(
            num_scalar_prefetch=1,
            grid=(8,),
            in_specs=[
                pl.BlockSpec((16, 16), lambda z, s: (0, 0)),
                pl.BlockSpec((16, 16), lambda z, s: (0, 0)),
                pl.BlockSpec((layers, 1, 128, width), lambda z, s: (0, z, 0, 0)),
            ],
            out_specs=[pl.BlockSpec((32, 1, 8, part), lambda z, s: (0, z, 0, 0))] * N_CHUNK,
        ),
        out_shape=[jax.ShapeDtypeStruct((32, 8, 8, part), BF16)] * N_CHUNK,
        cost_estimate=cost(2 * view.size, 4 * view.size),
    )(place, table, counts, view)


def combine_kernel(mods, arrived, out, acc):
    acc[...] = jnp.zeros_like(acc)
    for s in range(arrived.shape[0]):
        acc[mods[s]] += arrived[s, 0].astype(F32)
    out[0] = acc[...].astype(BF16)


def combine(mods, arrived):
    n, nz, rows, width = arrived.shape
    return pl.pallas_call(
        combine_kernel,
        name="combine",
        grid_spec=pltpu.PrefetchScalarGridSpec(
            num_scalar_prefetch=1,
            grid=(nz,),
            in_specs=[pl.BlockSpec((n, 1, rows, width), lambda z, s: (0, z, 0, 0))],
            out_specs=pl.BlockSpec((1, 16, rows, width), lambda z, s: (z, 0, 0, 0)),
            scratch_shapes=[pltpu.VMEM((16, rows, width), F32)],
        ),
        out_shape=jax.ShapeDtypeStruct((nz, 16, rows, width), BF16),
        cost_estimate=cost(arrived.size, 3 * arrived.size),
    )(mods, arrived)


def update_kernel(n, *refs):
    sums, outer, moment = refs[:n], refs[n], refs[n + 1]
    outer_out, moment_out, news = refs[n + 2], refs[n + 3], refs[n + 4 :]
    width = outer.shape[-1] // n
    for h in range(n):
        cols = pl.ds(h * width, width)
        for m in range(16):
            average = sums[h][m].astype(F32)
            parts = []
            for layer in range(2):
                old = outer[layer, m, :, cols]
                delta = old - average[layer * 4 : layer * 4 + 4]
                moved = 0.9 * moment[layer, m, :, cols] + delta
                new = old - 0.7 * (delta + 0.9 * moved)
                outer_out[layer, m, :, cols] = new
                moment_out[layer, m, :, cols] = moved
                parts.append(new)
            news[h][m] = jnp.concatenate(parts, axis=0).astype(BF16)


def update(sums, outer, moment):
    n = len(sums)
    vmem = pl.BlockSpec(memory_space=pltpu.VMEM)
    got = pl.pallas_call(
        functools.partial(update_kernel, n),
        name="update",
        in_specs=[vmem] * (n + 2),
        out_specs=[vmem] * (n + 2),
        out_shape=[jax.ShapeDtypeStruct(outer.shape, F32)] * 2
        + [jax.ShapeDtypeStruct(s.shape, BF16) for s in sums],
        cost_estimate=cost(8 * outer.size, 20 * outer.size),
    )(*sums, outer, moment)
    return got[0], got[1], got[2:]


def choose_kernel(mods, whole, out):
    for d in range(out.shape[0]):
        out[d, 0] = whole[0, mods[d]]


def choose(mods, whole):
    nz, _, rows, width = whole.shape
    return pl.pallas_call(
        choose_kernel,
        name="choose",
        grid_spec=pltpu.PrefetchScalarGridSpec(
            num_scalar_prefetch=1,
            grid=(nz,),
            in_specs=[pl.BlockSpec((1, 16, rows, width), lambda z, s: (z, 0, 0, 0))],
            out_specs=pl.BlockSpec((32, 1, rows, width), lambda z, s: (0, z, 0, 0)),
        ),
        out_shape=jax.ShapeDtypeStruct((32, nz, rows, width), BF16),
        cost_estimate=cost(0, 6 * whole.size),
    )(mods, whole)


def unpack_kernel(*refs):
    got, out = refs[:-1], refs[-1]
    width = out.shape[-1] // len(got)
    for yh in range(2):
        for pair in range(8):
            rows = pl.ds(yh * 64 + pair * 8, 8)
            for h, ref in enumerate(got):
                cols = pl.ds(h * width, width)
                even = ref[(2 * pair) * 2 + yh, 0].astype(F32)
                odd = ref[(2 * pair + 1) * 2 + yh, 0].astype(F32)
                first, second = swap_halves(even, odd)
                out[0, 0, rows, cols] = first.astype(BF16)
                out[1, 0, rows, cols] = second.astype(BF16)


def unpack(got, width):
    part = got[0].shape[-1]
    return pl.pallas_call(
        unpack_kernel,
        name="unpack",
        grid=(8,),
        in_specs=[pl.BlockSpec((32, 1, 8, part), lambda z: (0, z, 0, 0))] * len(got),
        out_specs=pl.BlockSpec((2, 1, 128, width), lambda z: (0, z, 0, 0)),
        out_shape=jax.ShapeDtypeStruct((2, 8, 128, width), BF16),
        cost_estimate=cost(0, 8 * width * width),
    )(*got).reshape(2, 1024, width)


def micro_step(tokens_path, params_path):
    state = tokens_path.astype(F32)
    for layer in range(params_path.shape[0]):
        scale = lax.rsqrt(jnp.mean(state * state, axis=-1, keepdims=True) + 1e-06)
        normed = (state * scale).astype(BF16)
        mixed = jnp.dot(normed, params_path[layer], preferred_element_type=F32)
        state = state + jax.nn.gelu(mixed, approximate=False)
    return state.astype(BF16)


def in_plane(blocks):
    return lax.all_to_all(blocks, PLANE, split_axis=0, concat_axis=0, tiled=True)


def on_device(tokens, local_params, outer_params, momentum, table, counts):
    row = lax.axis_index(("yl", "x", "core")).astype(jnp.int32)
    z = lax.axis_index("z").astype(jnp.int32)
    col = z * 2 + lax.axis_index("yh").astype(jnp.int32)
    place = jnp.stack([row, col])
    mods = lax.dynamic_slice(table, (0, z * 2), (16, 2)).reshape(32)
    params = local_params[0, 0]
    width = params.shape[-1]
    outer = outer_params.reshape(2, 16, 4, width)
    moment = momentum.reshape(2, 16, 4, width)
    packed = pack(place, table, counts, params)
    hidden = micro_step(tokens[0, 0], params)
    sums = []
    for chunk in packed:
        dense = combine(mods, in_plane(chunk))
        part = lax.psum_scatter(dense, "z", scatter_dimension=0, tiled=True)
        sums.append(part[0])
    outer_new, moment_new, news = update(sums, outer, moment)
    got = []
    for new in news:
        whole = lax.all_gather(new, "z", axis=0)
        got.append(in_plane(choose(mods, whole)))
    returned = unpack(got, width)
    return (
        returned[None, None],
        outer_new.reshape(outer_params.shape),
        moment_new.reshape(momentum.shape),
        hidden[None, None],
    )


def solution(mesh):
    devices = mesh.devices.reshape(2, 4, 2, 8, 2)
    fine = Mesh(devices, ("yl", "x", "core", "z", "yh"))
    row, col = ("yl", "x", "core"), ("z", "yh")
    return jax.shard_map(
        on_device,
        mesh=fine,
        in_specs=(
            P(row, col, None, None),
            P(row, col, None, None, None),
            P(None, None, col, row, None, None),
            P(None, None, col, row, None, None),
            P(),
            P(),
        ),
        out_specs=(
            P(row, col, None, None, None),
            P(None, None, col, row, None, None),
            P(None, None, col, row, None, None),
            P(row, col, None, None),
        ),
        check_vma=False,
    )
```

time: 382 us -> 258 us (0.68)
  blocking collectives: 54.5 us -> 0 us
  waiting for transfers between devices: 210 us -> 166 us
  local copies, waits for them, and re-layouts: 40.7 us -> 0.7 us
  Pallas kernels: 0 us -> 31.9 us
  other arithmetic: 20.2 us -> 0.96 us
    all_to_all x2, waiting for transfers between devices: 174 us -> 85.1 us  [in_plane(): lax.all_to_all(blocks, PLANE, split_axis=0, concat_axis=0, tiled=True)]
    all_to_all x1 -> x0, blocking collectives: 54.5 us -> none  [sum_at_owner(): lax.all_to_all(blocks, axis, split_axis=0, concat_axis=0, tiled=True)]
    reduce_scatter x0 -> x1, waiting for transfers between devices: none -> 42 us  [on_device(): part = lax.psum_scatter(dense, 'z', scatter_dimension=0, tiled=True)]
    pallas_call x0 -> x5, Pallas kernels: none -> 31.9 us  [the longest x1 8.53 us: pack(): pl.pallas_call(pack_kernel, name='pack', grid_spec=pltpu.PrefetchScalarGr...]
    reshape x2 -> x1, local copies, waits for them, and re-layouts: 11.8 us -> 0.61 us  [on_device(): mods = lax.dynamic_slice(table, (0, z * 2), (16, 2)).reshape(32)]
    gather x2 -> x0, local copies, waits for them, and re-layouts: 9.94 us -> none  [the longest x1 5.01 us: outer_round(): ordered = jnp.take(arrived, inverse, axis=1)]
    select_n x4 -> x0, other arithmetic: 9.34 us -> none  [the longest x2 4.67 us: outer_round(): ordered = jnp.take(arrived, inverse, axis=1)]
    all_gather x1 -> x0, local copies, waits for them, and re-layouts: 6.52 us -> none  [outer_round(): lax.all_gather(outer_new.astype(jnp.bfloat16), 'row', axis=2, tiled=True)]
  transfers between devices with their start and end apart: 3 -> 4, of which waited for: 3 -> 4; matrix products, arithmetic and copies ran while one was open for 6% -> 8% of each run, Pallas kernels for 0% -> 0%
where the time goes in v1:
time: 258 us; the launch traced here: 254 us
  waiting for transfers between devices  166 us (64%)
  Pallas kernels  31.9 us (12%)
  starting transfers between devices  20.6 us (8%)
  matrix products  19.4 us (8%)
  between operations  14.1 us (5%)
    all_to_all x2, waiting for transfers between devices, in_plane(): lax.all_to_all(blocks, PLANE, split_axis=0, concat_axis=0, tiled=True)  85.1 us
    reduce_scatter x1, waiting for transfers between devices, on_device(): part = lax.psum_scatter(dense, 'z', scatter_dimension=0, tiled=True)  42 us
    all_gather x1, waiting for transfers between devices, on_device(): whole = lax.all_gather(new, 'z', axis=0)  39.3 us
    all_to_all x2, starting transfers between devices, in_plane(): lax.all_to_all(blocks, PLANE, split_axis=0, concat_axis=0, tiled=True)  20.5 us
    dot_general x2, matrix products, micro_step(): mixed = jnp.dot(normed, params_path[layer], preferred_element_type=F32)  19.4 us
    pallas_call x1, Pallas kernels, pack(): pl.pallas_call(pack_kernel, name='pack', grid_spec=pltpu.PrefetchScalarGr...  8.53 us
    pallas_call x1, Pallas kernels, combine(): pl.pallas_call(combine_kernel, name='combine', grid_spec=pltpu.PrefetchSc...  7.38 us
    pallas_call x1, Pallas kernels, unpack(): pl.pallas_call(unpack_kernel, name='unpack', grid=(8,), in_specs=[pl.Bloc...  6.91 us
  transfers between devices with their start and end apart: 4, of which 4 were waited for; matrix products, arithmetic and copies ran while one was open for 8% of the time, Pallas kernels for 0%

profile of v1, /device:TPU:1, one launch (start us, length us, event | category | flops | bytes accessed | tf_op | source)
XLA Modules:
  0.0 254.2 jit_solution(1764931946876649610)
XLA Ops:
  7.2 0.6 pad_add_fusion.place
  7.8 8.5 %pack.1 = bf16[32,8,8,1024]{3,2,1,0:T(8,128)(2,1)} custom-call(s32[2]{0:T(128)} %pad_add_fusion.place, s32[16,16]{1,0:T(8,128)} %table.1, s32[16,16]{1,0:T(8,128)} %counts.1, bf16[2,8,128,1024]{3,2,1,0:T(8,128)(2,1)} %bitcast.45), custom_call_target="tpu_custom_call" | custom-call | flops 4194304 | bytes 8388608 | tf_op jit(solution)/shard_map/pack/pallas_call | solution.py:61
  16.3 0.0 copy-start.2
  16.3 8.8 %all-to-all-start = ((bf16[32,8,8,1024]{3,2,1,0:T(8,128)(2,1)}), bf16[32,8,8,1024]{3,2,1,0:T(8,128)(2,1)}, u32[]{:S(2)}, u32[]{:S(2)}) async-start(bf16[32,8,8,1024]{3,2,1,0:T(8,128)(2,1)} %pack.1), calls=%async_computation | async-start | bytes 8388608 | tf_op jit(solution)/shard_map/all_to_all | solution.py:198
  25.1 0.0 reduce-scatter.2.cloned.1.call-start
  25.1 0.0 copy-done.2
  25.1 0.1 constant_dynamic-slice_fusion
  25.2 0.6 reshape.53.mods
  25.8 51.9 %all-to-all-done.arrived = bf16[32,8,8,1024]{3,2,1,0:T(8,128)(2,1)} async-done(((bf16[32,8,8,1024]{3,2,1,0:T(8,128)(2,1)}), bf16[32,8,8,1024]{3,2,1,0:T(8,128)(2,1)}, u32[]{:S(2)}, u32[]{:S(2)}) %all-to-all-start) | async-done | bytes 4194336 | tf_op jit(solution)/shard_map/all_to_all | solution.py:198
  77.7 7.4 %combine.1 = bf16[8,16,8,1024]{3,2,1,0:T(8,128)(2,1)} custom-call(s32[32]{0:T(128)} %reshape.53.mods, bf16[32,8,8,1024]{3,2,1,0:T(8,128)(2,1)} %all-to-all-done.arrived), custom_call_target="tpu_custom_call" | custom-call | flops 2097152 | bytes 6291456 | tf_op jit(solution)/shard_map/combine/pallas_call | solution.py:88
  85.1 0.0 copy-start.1
  85.1 0.0 reduce-scatter.2.cloned.1.call-update
  85.1 0.0 all-gather.3.cloned.1.call-start
  85.2 42.0 %reduce-scatter.2.cloned.1.call-done = bf16[1,16,8,1024]{3,2,1,0:T(8,128)(2,1)} async-done(((bf16[8,16,8,1024]{3,2,1,0:T(8,128)(2,1)}), bf16[1,16,8,1024]{3,2,1,0:T(8,128)(2,1)}) %reduce-scatter.2.cloned.1.call-update) | async-done | bytes 262160 | tf_op jit(solution)/shard_map/reduce_scatter | solution.py:216
  127.2 2.4 update.1
  129.7 0.0 all-gather.3.cloned.1.call-update
  129.7 0.0 copy-done.1
  129.7 0.4 fusion.2
  130.1 39.3 %all-gather.3.cloned.1.call-done = bf16[128,8,1024]{2,1,0:T(8,128)(2,1)} async-done(((bf16[16,8,1024]{2,1,0:T(8,128)(2,1)}), bf16[128,8,1024]{2,1,0:T(8,128)(2,1)}) %all-gather.3.cloned.1.call-update) | async-done | bytes 2097168 | tf_op jit(solution)/shard_map/all_gather | solution.py:221
  169.3 6.6 %choose.1 = bf16[32,8,8,1024]{3,2,1,0:T(8,128)(2,1)} custom-call(s32[32]{0:T(128)} %reshape.53.mods, bf16[8,16,8,1024]{3,2,1,0:T(8,128)(2,1)} %bitcast.47), custom_call_target="tpu_custom_call" | custom-call | bytes 6291456 | tf_op jit(solution)/shard_map/choose/pallas_call | solution.py:145
  176.0 11.8 %all-to-all-start.1 = ((bf16[32,8,8,1024]{3,2,1,0:T(8,128)(2,1)}), bf16[32,8,8,1024]{3,2,1,0:T(8,128)(2,1)}, u32[]{:S(2)}, u32[]{:S(2)}) async-start(bf16[32,8,8,1024]{3,2,1,0:T(8,128)(2,1)} %choose.1), calls=%async_computation.2 | async-start | bytes 8388608 | tf_op jit(solution)/shard_map/all_to_all | solution.py:198
  187.8 0.0 copy-start
  187.8 10.1 %multiply_reduce_fusion = (f32[736]{0:T(1024)S(1)}, f32[736,1024]{1,0:T(8,128)S(1)}) fusion(bf16[1,1,2,1024,1024]{4,3,2,1,0:T(8,128)(2,1)} %param.7, bf16[1,1,736,1024]{3,2,1,0:T(8,128)(2,1)S(1)} %copy-done.1, f32[736]{0:T(1024)S(1)} %add_rsqrt_fusion.1), kind=kOutput, calls=%fused_computation.28 | convolution fusion | flops 1597013248 | bytes 8133504 | tf_op jit(solution)/shard_map/dot_general | solution.py:192
  197.9 0.0 copy-done
  197.9 9.4 %fusion.36 = bf16[1,1,736,1024]{3,2,1,0:T(8,128)(2,1)} fusion(f32[736,1024]{1,0:T(8,128)S(1)} %get-tuple-element.23, bf16[1,1,2,1024,1024]{4,3,2,1,0:T(8,128)(2,1)S(1)} %copy-done, f32[736]{0:T(1024)S(1)} %add_rsqrt_fusion), kind=kOutput, calls=%fused_computation.55 | convolution fusion | flops 1594753024 | bytes 9637888 | tf_op jit(solution)/shard_map/dot_general | solution.py:192
  207.2 33.2 %all-to-all-done.1.refs_0_ = bf16[32,8,8,1024]{3,2,1,0:T(8,128)(2,1)} async-done(((bf16[32,8,8,1024]{3,2,1,0:T(8,128)(2,1)}), bf16[32,8,8,1024]{3,2,1,0:T(8,128)(2,1)}, u32[]{:S(2)}, u32[]{:S(2)}) %all-to-all-start.1) | async-done | bytes 4194336 | tf_op jit(solution)/shard_map/all_to_all | solution.py:198
  240.4 6.9 %unpack.1 = bf16[2,8,128,1024]{3,2,1,0:T(8,128)(2,1)} custom-call(bf16[32,8,8,1024]{3,2,1,0:T(8,128)(2,1)} %all-to-all-done.1.refs_0_), custom_call_target="tpu_custom_call" | custom-call | bytes 8388608 | tf_op jit(solution)/shard_map/unpack/pallas_call | solution.py:176
  (2 shorter events, 0.0 us)
Async XLA Ops:
  16.3 8.8 %copy-start.2 = (s32[16,16]{1,0:T(8,128)S(1)}, s32[16,16]{1,0:T(8,128)}, u32[]{:S(2)}) copy-start(s32[16,16]{1,0:T(8,128)} %table.1) | copy-start | bytes 3076
  16.3 61.4 %all-to-all-start = ((bf16[32,8,8,1024]{3,2,1,0:T(8,128)(2,1)}), bf16[32,8,8,1024]{3,2,1,0:T(8,128)(2,1)}, u32[]{:S(2)}, u32[]{:S(2)}) async-start(bf16[32,8,8,1024]{3,2,1,0:T(8,128)(2,1)} %pack.1), calls=%async_computation | async-start | bytes 8388608 | tf_op jit(solution)/shard_map/all_to_all | solution.py:198
  25.1 102.1 %reduce-scatter.2.cloned.1.call-start = ((), (), s32[]{:S(2)}) async-start(), calls=%async_computation.3 | async-start | bytes 2359296 | tf_op jit(solution)/shard_map/reduce_scatter | solution.py:216
  85.1 44.6 %copy-start.1 = (bf16[1,1,736,1024]{3,2,1,0:T(8,128)(2,1)S(1)}, bf16[1,1,736,1024]{3,2,1,0:T(8,128)(2,1)}, u32[]{:S(2)}) copy-start(bf16[1,1,736,1024]{3,2,1,0:T(8,128)(2,1)} %param.6) | copy-start | bytes 4521988
  85.1 84.2 %all-gather.3.cloned.1.call-start = ((), (), s32[]{:S(2)}) async-start(), calls=%async_computation.4 | async-start | bytes 2359296 | tf_op jit(solution)/shard_map/all_gather | solution.py:221
  176.0 64.4 %all-to-all-start.1 = ((bf16[32,8,8,1024]{3,2,1,0:T(8,128)(2,1)}), bf16[32,8,8,1024]{3,2,1,0:T(8,128)(2,1)}, u32[]{:S(2)}, u32[]{:S(2)}) async-start(bf16[32,8,8,1024]{3,2,1,0:T(8,128)(2,1)} %choose.1), calls=%async_computation.2 | async-start | bytes 8388608 | tf_op jit(solution)/shard_map/all_to_all | solution.py:198
  187.8 10.1 %copy-start = (bf16[1,1,2,1024,1024]{4,3,2,1,0:T(8,128)(2,1)S(1)}, bf16[1,1,2,1024,1024]{4,3,2,1,0:T(8,128)(2,1)}, u32[]{:S(2)}) copy-start(bf16[1,1,2,1024,1024]{4,3,2,1,0:T(8,128)(2,1)} %param.7) | copy-start | bytes 12582916
Sparse Core Ops, SparseCore 0:
  85.2 41.9 reduce-scatter.1
  129.8 39.5 all-gather.2
